TPU v7x, 32 devices: a whole 2x2x4 slice. The times are simulated.
32 devices in a mesh: lat: 8 (over z, x), lev: 4 (over y, core).
Axes of the slice: x: 2, y: 2, z: 4, core: 2. Of those that a mesh axis runs over, the one named last changes fastest.
Arguments:
- pressure_thick: float32 [16, 192, 1152], P('lev', 'lat'), may hold values from 0.016 to 4.7
- potential_temp: float32 [16, 192, 1152], P('lev', 'lat'), may hold values from 0.5 to 3
- tracer: float32 [16, 192, 1152], P('lev', 'lat'), may hold values from 0 to 1
- east_courant: float32 [16, 192, 1152], P('lev', 'lat'), may hold values from -0.15 to 0.15
- north_courant: float32 [16, 192, 1152], P('lev', 'lat'), may hold values from -0.15 to 0.15
- polar_mask: int32 [192], P('lat'), may hold values from 0 to 1, as said below
- wave_cutoff: int32 [192], P('lat'), may hold values from 1 to 576, as said below
- level_weight: float32 [16], replicated, may hold values from 0.3 to 3
- target_surface: float32 [1], replicated, may hold values from 16 to 22.4
Outputs:
- remapped_thick: float32 [16, 192, 1152], P(None, 'lev', 'lat')
- remapped_temp: float32 [16, 192, 1152], P(None, 'lev', 'lat')
- remapped_tracer: float32 [16, 192, 1152], P(None, 'lev', 'lat')
Inputs may be any that keep to these rules, and one draw needn't show every extreme that they name: `polar_mask`: 1 on the first and last P rows and 0 between, for one P from 24 to 38. `wave_cutoff`: rows with polar_mask 0 hold 576.
All inputs are finite; a program needn't handle non-finite values.
Results may differ from a plain program's by a relative error of at most 0.0003.
Values sent between devices are 32-bit elements; how exact they have to be, the bound alone decides.
A program may use at most 128 MiB of HBM per device.

v0:
```python
import functools
import math

import jax
import jax.numpy as jnp
import numpy as np
from jax import lax
from jax.experimental import pallas as pl
from jax.experimental.pallas import tpu as pltpu
from jax.sharding import PartitionSpec as P

LANES = 128
SUB = 8
VMEM = pl.BlockSpec(memory_space=pltpu.VMEM)
SMEM = pl.BlockSpec(memory_space=pltpu.SMEM)
MESH = pl.DeviceIdType.MESH


@functools.cache
def dft_tables(nlon):
    radix = nlon // LANES
    b = np.arange(LANES)[:, None]
    k2 = np.arange(LANES)[None, :]
    high, low = [], []
    for k1 in range(radix // 2 + 1):
        phase = (b * (k1 + radix * k2) % nlon) * (2.0 * np.pi / nlon)
        c, s = np.cos(phase), np.sin(phase)
        table = np.block([[c, -s], [s, c]]).astype(np.float32)
        top = table.astype(jnp.bfloat16)
        high.append(top)
        low.append((table - top.astype(np.float32)).astype(jnp.bfloat16))
    return np.stack(high), np.stack(low)


@functools.cache
def row_tables(nlat):
    rows = np.arange(nlat, dtype=np.float64)
    out = np.zeros((nlat, LANES), np.float32)
    out[:, 0] = np.sin((rows + 0.5) * np.pi / nlat)
    out[:, 1] = 1.0 / np.sin((rows + 0.5) * np.pi / nlat)
    out[:, 2] = np.sin((rows + 1.0) * np.pi / nlat)
    out[:, 3] = np.sin(rows * np.pi / nlat)
    return out


def pack_plan(width, groups):
    full, rest = divmod(width, LANES)
    cap = LANES // rest if rest else 1
    tail_tiles = -(-groups // cap) if rest else 0
    return full, rest, cap, tail_tiles


def split_bf16(x):
    top = x.astype(jnp.bfloat16)
    return top, (x - top.astype(jnp.float32)).astype(jnp.bfloat16)


def update_kernel(
    n_lat,
    p_ref, t_ref, q_ref, e_ref, n_ref, south_ref, north_ref, mask_ref, cut_ref,
    rows_ref, mh_ref, ml_ref,
    send_ref, part_ref,
    tend, spec, new, yh, yl,
):
    levs, lats, nlon = p_ref.shape
    radix = nlon // LANES
    half = radix // 2
    first = pl.multiple_of(lax.axis_index("lat") * lats, SUB)
    table = rows_ref[pl.ds(first, lats), :]
    cc, icc, face, face_s = (table[:, c : c + 1] for c in range(4))
    face_s = face_s[0:1]
    row = lax.broadcasted_iota(jnp.int32, (lats, nlon), 0)

    def up(x, halo):
        return jnp.where(row == lats - 1, halo, pltpu.roll(x, lats - 1, 0))

    def down(x, halo):
        return jnp.where(row == 0, halo, pltpu.roll(x, 1, 0))

    def east(x):
        return pltpu.roll(x, nlon - 1, 1)

    def west(x):
        return pltpu.roll(x, 1, 1)

    @pl.loop(0, levs)
    def _(l):
        p, t, q, ec, nc = (r[l] for r in (p_ref, t_ref, q_ref, e_ref, n_ref))
        em = ec * (p + east(p)) * 0.5
        nm = nc * (p + up(p, north_ref[l, 0:1])) * 0.5 * face
        sm = south_ref[l, 3:4] * (south_ref[l, 0:1] + p[0:1]) * 0.5 * face_s
        base = pl.multiple_of(l * 3 * lats, SUB)
        tend[pl.ds(base, lats)] = -((em - west(em)) + (nm - down(nm, sm)) * icc)
        for f, s in ((1, t), (2, q)):
            es = em * (s + east(s)) * 0.5
            ns = nm * (s + up(s, north_ref[l, f : f + 1])) * 0.5
            ss = sm * (south_ref[l, f : f + 1] + s[0:1]) * 0.5
            tend[pl.ds(pl.multiple_of(base + f * lats, SUB), lats)] = -(
                (es - west(es)) + (ns - down(ns, ss)) * icc
            )

    total_rows = tend.shape[0]
    block = 32 if total_rows % 32 == 0 else 16

    @pl.loop(0, total_rows // block)
    def _(rb):
        at = pl.ds(pl.multiple_of(rb * block, 16), block)
        c = [tend[at, a * LANES : (a + 1) * LANES] for a in range(radix)]
        s = [c[a] + c[radix - a] for a in range(1, half + 1)]
        d = [c[a] - c[radix - a] for a in range(1, half + 1)]
        for k1 in range(half + 1):
            re = c[0]
            im = None
            for a in range(1, half + 1):
                angle = 2.0 * math.pi * (a * k1 % radix) / radix
                re = re + s[a - 1] * math.cos(angle)
                if k1:
                    term = d[a - 1] * -math.sin(angle)
                    im = term if im is None else im + term
            lo = 0 if k1 == 0 else LANES + (k1 - 1) * 2 * LANES
            h, w = split_bf16(re)
            yh[at, lo : lo + LANES] = h
            yl[at, lo : lo + LANES] = w
            if k1:
                h, w = split_bf16(im)
                yh[at, lo + LANES : lo + 2 * LANES] = h
                yl[at, lo + LANES : lo + 2 * LANES] = w

    sub_row = lax.broadcasted_iota(jnp.int32, (lats, 2 * LANES), 0)
    cuts = jnp.full((lats, 2 * LANES), nlon, jnp.int32)
    for r in range(lats):
        value = jnp.where(mask_ref[r] > 0, cut_ref[r], nlon)
        cuts = jnp.where(sub_row == r, value, cuts)
    k2 = lax.broadcasted_iota(jnp.int32, (lats, 2 * LANES), 1) % LANES

    dot = functools.partial(jnp.dot, preferred_element_type=jnp.float32)

    def dot_t(a, b):
        return lax.dot_general(a, b, (((1,), (1,)), ((), ())), preferred_element_type=jnp.float32)

    for k1 in range(half + 1):
        lo = 0 if k1 == 0 else LANES + (k1 - 1) * 2 * LANES
        size = LANES if k1 == 0 else 2 * LANES
        mh, ml = mh_ref[k1, :size], ml_ref[k1, :size]
        h, w = yh[:, lo : lo + size], yl[:, lo : lo + size]
        x = dot(h, mh) + dot(h, ml) + dot(w, mh)
        k = k1 + radix * k2
        wave = jnp.minimum(k, nlon - k)
        keep = jnp.where(wave >= cuts, (1.0 if k1 == 0 else 2.0) / nlon, 0.0)
        x = (x.reshape(-1, lats, 2 * LANES) * keep[None]).reshape(-1, 2 * LANES)
        h, w = split_bf16(x)
        spec[:, lo : lo + size] = dot_t(h, mh) + dot_t(h, ml) + dot_t(w, mh)

    part_ref[...] = jnp.zeros_like(part_ref)

    @pl.loop(0, levs)
    def _(l):
        base = pl.multiple_of(l * 3 * lats, SUB)

        def filtered(f):
            at = pl.ds(pl.multiple_of(base + f * lats, SUB), lats)
            z0 = spec[at, 0:LANES]
            re = [spec[at, (2 * k - 1) * LANES : 2 * k * LANES] for k in range(1, half + 1)]
            im = [spec[at, 2 * k * LANES : (2 * k + 1) * LANES] for k in range(1, half + 1)]
            parts = [None] * radix
            for a in range(half + 1):
                even, odd = z0, None
                for k in range(1, half + 1):
                    angle = 2.0 * math.pi * (a * k % radix) / radix
                    even = even + re[k - 1] * math.cos(angle)
                    if a:
                        term = im[k - 1] * math.sin(angle)
                        odd = term if odd is None else odd + term
                if a:
                    parts[a] = even - odd
                    parts[radix - a] = even + odd
                else:
                    parts[0] = even
            return tend[at] - jnp.concatenate(parts, axis=1)

        p, t, q = p_ref[l], t_ref[l], q_ref[l]
        fm = filtered(0)
        np_ = p + fm
        inv = 1.0 / p
        new[pl.ds(base, lats)] = np_
        area = np_ * cc
        acc = part_ref[...]
        for g in range(lats // SUB):
            for a in range(radix):
                acc = acc + area[g * SUB : (g + 1) * SUB, a * LANES : (a + 1) * LANES]
        part_ref[...] = acc
        for f, s in ((1, t), (2, q)):
            new[pl.ds(pl.multiple_of(base + f * lats, SUB), lats)] = s + (filtered(f) - s * fm) * inv

    width = nlon // n_lat
    groups = total_rows // SUB
    full, rest, cap, tail_tiles = pack_plan(width, groups)
    lane = lax.broadcasted_iota(jnp.int32, (SUB, LANES), 1)
    for j in range(n_lat):
        t0, off = divmod(width * j, LANES)
        nt = -(-(off + width) // LANES)
        acc = None
        for g in range(groups):
            x = new[g * SUB : (g + 1) * SUB, t0 * LANES : (t0 + nt) * LANES]
            if off:
                x = pltpu.roll(x, nt * LANES - off, 1)
            for a in range(full):
                send_ref[j, (a * groups + g) * SUB : (a * groups + g + 1) * SUB, :] = x[
                    :, a * LANES : (a + 1) * LANES
                ]
            if rest:
                slot = g % cap
                y = x[:, full * LANES : (full + 1) * LANES]
                if slot:
                    y = pltpu.roll(y, slot * rest, 1)
                acc = y if slot == 0 else jnp.where(lane >= slot * rest, y, acc)
                if slot == cap - 1 or g == groups - 1:
                    o = (full * groups + g // cap) * SUB
                    send_ref[j, o : o + SUB, :] = acc


def exchange_kernel(
    n_lat, n_lev,
    send_ref, part_ref,
    out_ref, sums_ref,
    mid, s1, r1, s2, r2, local, sa, ra, sb, rb,
):
    per = n_lat // n_lev
    i = lax.axis_index("lat")
    l = lax.axis_index("lev")
    owner = i // per
    barrier = pltpu.get_barrier_semaphore()
    for d in range(1, n_lat):
        pl.semaphore_signal(barrier, 1, device_id=((i + d) % n_lat, l), device_id_type=MESH)
    for d in range(1, n_lev):
        pl.semaphore_signal(barrier, 1, device_id=(i, (l + d) % n_lev), device_id_type=MESH)
    pl.semaphore_wait(barrier, n_lat - 1 + n_lev - 1)

    order = sorted(range(1, n_lat), key=lambda d: abs(d - n_lat / 2))

    def remote(src, dst, ss, rs, dev):
        return pltpu.make_async_remote_copy(
            src_ref=src, dst_ref=dst, send_sem=ss, recv_sem=rs, device_id=dev, device_id_type=MESH
        )

    def stage1(d, direct):
        dst = out_ref.at[l * per + i % per] if direct else mid.at[d]
        j = (i + d) % n_lat
        return remote(send_ref.at[j], dst, s1.at[d], r1.at[d], (j, l))

    def sums_a(d):
        j = (i + d) % n_lat
        return remote(part_ref, sums_ref.at[l, i], sa.at[d], ra.at[d], (j, l))

    def sums_b(d):
        return remote(sums_ref.at[l], sums_ref.at[l], sb.at[d], rb.at[d], (i, (l + d) % n_lev))

    own_part = pltpu.make_async_copy(part_ref, sums_ref.at[l, i], local.at[1])
    own_part.start()
    for d in order:
        sums_a(d).start()

    @pl.when(owner == l)
    def _():
        for d in order:
            stage1(d, True).start()
        pltpu.make_async_copy(send_ref.at[i], out_ref.at[l * per + i % per], local.at[0]).start()

    def stage2(d, src_lat, src):
        slot = l * per + src_lat % per
        return remote(src, out_ref.at[slot], s2.at[d], r2.at[slot], (i, src_lat // per))

    @pl.when(owner != l)
    def _():
        for d in order:
            stage1(d, False).start()
        stage2(0, i, send_ref.at[i]).start()

    own_part.wait()
    for d in order:
        sums_a(d).wait_recv()
    for d in range(1, n_lev):
        sums_b(d).start()

    for d in order:
        src_lat = (i + n_lat - d) % n_lat
        stage1(d, False).wait_recv()

        @pl.when(src_lat // per != l)
        def _():
            stage2(d, src_lat, mid.at[d]).start()

    for e in range(1, n_lev):
        for r in range(per):
            slot = ((l + e) % n_lev) * per + r
            remote(mid.at[0], out_ref.at[slot], s2.at[0], r2.at[slot], (i, l)).wait_recv()
    for d in range(1, n_lev):
        sums_b(d).wait_recv()

    for d in order:
        src_lat = (i + n_lat - d) % n_lat
        stage1(d, False).wait_send()
        sums_a(d).wait_send()

        @pl.when(src_lat // per != l)
        def _():
            stage2(d, src_lat, mid.at[d]).wait_send()

    for d in range(1, n_lev):
        sums_b(d).wait_send()

    @pl.when(owner == l)
    def _():
        pltpu.make_async_copy(send_ref.at[i], out_ref.at[l * per + i % per], local.at[0]).wait()

    @pl.when(owner != l)
    def _():
        stage2(0, i, send_ref.at[i]).wait_send()


def remap_kernel(
    n_lat, n_lev, lats, nlon, area_total,
    got_ref, sums_ref, weight_ref, target_ref,
    thick_out, temp_out, tracer_out,
    cols, share, res,
):
    per = n_lat // n_lev
    levels = thick_out.shape[0]
    levs = levels // n_lev
    rgs = lats // SUB
    width = nlon // n_lat
    groups = levs * 3 * rgs
    full, rest, cap, tail_tiles = pack_plan(width, groups)
    lane = lax.broadcasted_iota(jnp.int32, (SUB, LANES), 1)
    outs = (thick_out, temp_out, tracer_out)

    whole = jnp.full((SUB, LANES), weight_ref[0])
    for k in range(1, levels):
        whole = whole + weight_ref[k]
    run = jnp.zeros((SUB, LANES), jnp.float32)
    for k in range(levels):
        part = jnp.full((SUB, LANES), weight_ref[k]) / whole
        run = run + part
        share[0, k] = part
        share[1, k] = run
        share[2, k] = 1.0 / part
    sums = sums_ref[...].reshape(-1, SUB, LANES)
    total = jnp.sum(jnp.sum(sums, axis=0), keepdims=True)
    factor = jnp.full((1, 1), target_ref[0] * (nlon * area_total)) / total

    n_main = full * per * rgs
    col_groups = per * rgs
    for lev in range(n_lev):
        for ll in range(levs):
            for f in range(3):
                acc = None
                for rs in range(per):
                    for rg in range(rgs):
                        g = (ll * 3 + f) * rgs + rg
                        for a in range(full):
                            v = (a * per + rs) * rgs + rg
                            o = (a * groups + g) * SUB
                            cols[f, lev * levs + ll, v] = got_ref[lev * per + rs, o : o + SUB, :]
                        if rest:
                            o = (full * groups + g // cap) * SUB
                            y = got_ref[lev * per + rs, o : o + SUB, :]
                            cg = rs * rgs + rg
                            slot = cg % cap
                            shift = (slot - g % cap) * rest % LANES
                            if shift:
                                y = pltpu.roll(y, shift, 1)
                            acc = (
                                y if slot == 0
                                else jnp.where(lane >= slot * rest, y, acc)
                            )
                            if slot == cap - 1 or cg == col_groups - 1:
                                last = (slot + 1) * rest
                                if last < LANES:
                                    acc = jnp.where(lane < last, acc, 1.0)
                                cols[f, lev * levs + ll, n_main + cg // cap] = acc

    def remap(v, put):
        thick = [cols[0, m, v] for m in range(levels)]
        tops = []
        surface = jnp.zeros((SUB, LANES), jnp.float32)
        for m in range(levels):
            tops.append(surface)
            surface = surface + thick[m]
        inv = 1.0 / surface
        scale = surface * factor
        before = (jnp.zeros_like(surface), jnp.zeros_like(surface))
        for k in range(levels):
            bound = surface * share[1, k]
            ct = cq = None
            for m in range(levels):
                w = jnp.minimum(jnp.maximum(bound - tops[m], 0.0), thick[m])
                dt, dq = cols[1, m, v] * w, cols[2, m, v] * w
                ct, cq = (dt, dq) if m == 0 else (ct + dt, cq + dq)
            per_share = inv * share[2, k]
            put(k, scale * share[0, k], (ct - before[0]) * per_share, (cq - before[1]) * per_share)
            before = (ct, cq)

    if full:
        for a in range(full):
            @pl.loop(0, col_groups)
            def _(v):
                at = pl.ds(pl.multiple_of(v * SUB, SUB), SUB)

                def put(k, *values):
                    for ref, x in zip(outs, values):
                        ref[k, at, a * LANES : (a + 1) * LANES] = x

                remap(a * col_groups + v, put)

    if rest:
        n_tail = -(-col_groups // cap)

        @pl.loop(0, n_tail)
        def _(v):
            def put(k, *values):
                for f, x in enumerate(values):
                    res[f, k, v] = x

            remap(n_main + v, put)

        for cg in range(col_groups):
            @pl.loop(0, levels)
            def _(k):
                for f in range(3):
                    x = res[f, k, cg // cap]
                    if cg % cap:
                        x = pltpu.roll(x, LANES - (cg % cap) * rest, 1)
                    outs[f][k, cg * SUB : (cg + 1) * SUB, full * LANES : full * LANES + rest] = x[:, :rest]


def on_device(p, t, q, ec, nc, polar_mask, wave_cutoff, level_weight, target_surface):
    levs, lats, nlon = p.shape
    n_lat, n_lev = lax.axis_size("lat"), lax.axis_size("lev")
    nlat = lats * n_lat
    levels = levs * n_lev
    per = n_lat // n_lev
    width = nlon // n_lat
    f32 = jnp.float32
    tail = jnp.stack([p[:, -1], t[:, -1], q[:, -1], nc[:, -1]], axis=1)
    head = jnp.stack([p[:, 0], t[:, 0], q[:, 0]], axis=1)
    south = lax.ppermute(tail, "lat", [(i, i + 1) for i in range(n_lat - 1)])
    north = lax.ppermute(head, "lat", [(i + 1, i) for i in range(n_lat - 1)])
    high, low = dft_tables(nlon)
    rows = levs * 3 * lats
    groups = rows // SUB
    full, rest, cap, tail_tiles = pack_plan(width, groups)
    packed = (full * groups + tail_tiles) * SUB
    limit = pltpu.CompilerParams(vmem_limit_bytes=48 * 1024 * 1024)
    send, part = pl.pallas_call(
        functools.partial(update_kernel, n_lat),
        out_shape=(
            jax.ShapeDtypeStruct((n_lat, packed, LANES), f32),
            jax.ShapeDtypeStruct((SUB, LANES), f32),
        ),
        in_specs=[VMEM] * 7 + [SMEM] * 2 + [VMEM] * 3,
        out_specs=(VMEM, VMEM),
        scratch_shapes=[
            pltpu.VMEM((rows, nlon), f32),
            pltpu.VMEM((rows, nlon), f32),
            pltpu.VMEM((rows, nlon), f32),
            pltpu.VMEM((rows, nlon), jnp.bfloat16),
            pltpu.VMEM((rows, nlon), jnp.bfloat16),
        ],
        compiler_params=limit,
        name="update",
    )(p, t, q, ec, nc, south, north, polar_mask, wave_cutoff, jnp.asarray(row_tables(nlat)),
      jnp.asarray(high), jnp.asarray(low))

    dma = pltpu.SemaphoreType.DMA
    got, sums = pl.pallas_call(
        functools.partial(exchange_kernel, n_lat, n_lev),
        out_shape=(
            jax.ShapeDtypeStruct((n_lev * per, packed, LANES), f32),
            jax.ShapeDtypeStruct((n_lev, n_lat, SUB, LANES), f32),
        ),
        in_specs=[VMEM, VMEM],
        out_specs=(VMEM, VMEM),
        scratch_shapes=[
            pltpu.VMEM((n_lat, packed, LANES), f32),
            dma((n_lat,)), dma((n_lat,)), dma((n_lat,)), dma((n_lev * per,)), dma((2,)),
            dma((n_lat,)), dma((n_lat,)), dma((n_lev,)), dma((n_lev,)),
        ],
        compiler_params=pltpu.CompilerParams(
            collective_id=0, has_side_effects=True, vmem_limit_bytes=32 * 1024 * 1024
        ),
        name="exchange",
    )(send, part)

    area_total = float(np.sum(np.sin((np.arange(nlat) + 0.5) * np.pi / nlat)))
    col_groups = per * lats // SUB
    n_tail = -(-col_groups // cap) if rest else 0
    out = jax.ShapeDtypeStruct((levels, nlat // n_lev, width), f32)
    return pl.pallas_call(
        functools.partial(remap_kernel, n_lat, n_lev, lats, nlon, area_total),
        out_shape=(out, out, out),
        in_specs=[VMEM, VMEM, SMEM, SMEM],
        out_specs=(VMEM, VMEM, VMEM),
        scratch_shapes=[
            pltpu.VMEM((3, levels, full * col_groups + n_tail, SUB, LANES), f32),
            pltpu.VMEM((3, levels, SUB, LANES), f32),
            pltpu.VMEM((3, levels, max(n_tail, 1), SUB, LANES), f32),
        ],
        compiler_params=limit,
        name="remap",
    )(got, sums, level_weight, target_surface)


def solution(mesh):
    return jax.shard_map(
        on_device,
        mesh=mesh,
        in_specs=(P("lev", "lat", None),) * 5 + (P("lat"), P("lat"), P(), P()),
        out_specs=(P(None, "lev", "lat"),) * 3,
        check_vma=False,
    )
```

profile of v0, /device:TPU:0, one launch (start us, length us, event | category | flops | bytes accessed | tf_op | source)
XLA Modules:
  0.0 94.0 jit_solution(9328535366179295303)
XLA Ops:
  0.6 0.9 slice.24
  1.6 1.0 %fusion.2 = (f32[4,1,1152]{2,1,0:T(1,128)S(1)}, f32[4,1,1152]{2,1,0:T(1,128)S(1)}) fusion(f32[4,24,1152]{2,1,0:T(8,128)} %q_ref.1), kind=kLoop, calls=%fused_computation.4 | loop fusion | bytes 73728 | tf_op jit(solution)/shard_map/slice | solution.py:445
  2.6 1.2 %fusion = (f32[4,1,1152]{2,1,0:T(1,128)S(1)}, f32[4,1,1152]{2,1,0:T(1,128)S(1)}, f32[4,1,1152]{2,1,0:T(1,128)S(1)}, f32[4,1,1152]{2,1,0:T(1,128)S(1)}) fusion(f32[4,24,1152]{2,1,0:T(8,128)} %p_ref.1, f32[4,24,1152]{2,1,0:T(8,128)} %t_ref.1), kind=kLoop, calls=%fused_computation.2 | loop fusion | bytes 147456 | tf_op jit(solution)/shard_map/slice | solution.py:445
  3.8 0.1 pad_maximum_fusion
  3.8 4.9 %collective-permute-start = (f32[4,4,1152]{2,1,0:T(4,128)S(1)}, f32[4,4,1152]{2,1,0:T(4,128)S(1)}, u32[]{:S(2)}, u32[]{:S(2)}) collective-permute-start(f32[4,4,1152]{2,1,0:T(4,128)S(1)} %pad_maximum_fusion), channel_id=1, source_target_pairs={{0,4},{4,8},{8,12},{12,16},{16,20},{20,24},{24,28},{1,5},{5,9},{9,... | collective-permute-start | bytes 221192 | tf_op jit(solution)/shard_map/ppermute | solution.py:446
  8.7 0.1 pad_maximum_fusion.1
  8.8 1.3 %collective-permute-start.1 = (f32[4,3,1152]{2,1,0:T(4,128)S(1)}, f32[4,3,1152]{2,1,0:T(4,128)S(1)}, u32[]{:S(2)}, u32[]{:S(2)}) collective-permute-start(f32[4,3,1152]{2,1,0:T(4,128)S(1)} %pad_maximum_fusion.1), channel_id=1, source_target_pairs={{4,0},{8,4},{12,8},{16,12},{20,16},{24,20},{28,24},{5,1},{9,5},{13... | collective-permute-start | bytes 165896 | tf_op jit(solution)/shard_map/ppermute | solution.py:447
  10.7 4.3 %collective-permute-done.1.north_ref = f32[4,3,1152]{2,1,0:T(4,128)S(1)} collective-permute-done((f32[4,3,1152]{2,1,0:T(4,128)S(1)}, f32[4,3,1152]{2,1,0:T(4,128)S(1)}, u32[]{:S(2)}, u32[]{:S(2)}) %collective-permute-start.1) | collective-permute-done | bytes 55328 | tf_op jit(solution)/shard_map/ppermute | solution.py:447
  15.0 0.0 collective-permute-done.south_ref
  15.0 1.1 %copy-done = bf16[5,256,256]{2,1,0:T(8,128)(2,1)S(1)} copy-done((bf16[5,256,256]{2,1,0:T(8,128)(2,1)S(1)}, bf16[5,256,256]{2,1,0:T(8,128)(2,1)}, u32[]{:S(2)}) %copy-start) | copy-done | bytes 655384
  16.1 1.1 %copy-done.1 = bf16[5,256,256]{2,1,0:T(8,128)(2,1)S(1)} copy-done((bf16[5,256,256]{2,1,0:T(8,128)(2,1)S(1)}, bf16[5,256,256]{2,1,0:T(8,128)(2,1)}, u32[]{:S(2)}) %copy-start.1) | copy-done | bytes 655384
  17.2 1.0 %copy-done.2 = f32[4,24,1152]{2,1,0:T(8,128)S(1)} copy-done((f32[4,24,1152]{2,1,0:T(8,128)S(1)}, f32[4,24,1152]{2,1,0:T(8,128)}, u32[]{:S(2)}) %copy-start.2) | copy-done | bytes 442392
  18.2 1.0 %copy-done.3 = f32[4,24,1152]{2,1,0:T(8,128)S(1)} copy-done((f32[4,24,1152]{2,1,0:T(8,128)S(1)}, f32[4,24,1152]{2,1,0:T(8,128)}, u32[]{:S(2)}) %copy-start.3) | copy-done | bytes 442392
  19.2 1.0 %copy-done.4 = f32[4,24,1152]{2,1,0:T(8,128)S(1)} copy-done((f32[4,24,1152]{2,1,0:T(8,128)S(1)}, f32[4,24,1152]{2,1,0:T(8,128)}, u32[]{:S(2)}) %copy-start.4) | copy-done | bytes 442392
  20.3 1.0 %copy-done.5 = f32[4,24,1152]{2,1,0:T(8,128)S(1)} copy-done((f32[4,24,1152]{2,1,0:T(8,128)S(1)}, f32[4,24,1152]{2,1,0:T(8,128)}, u32[]{:S(2)}) %copy-start.5) | copy-done | bytes 442392
  21.3 1.0 %copy-done.6 = f32[4,24,1152]{2,1,0:T(8,128)S(1)} copy-done((f32[4,24,1152]{2,1,0:T(8,128)S(1)}, f32[4,24,1152]{2,1,0:T(8,128)}, u32[]{:S(2)}) %copy-start.6) | copy-done | bytes 442392
  22.3 0.9 copy-done.7
  23.2 0.7 copy-done.9
  23.8 0.7 copy-done.10
  24.5 18.4 %update.1 = (f32[8,328,128]{2,1,0:T(8,128)S(1)}, f32[8,128]{1,0:T(8,128)S(1)}) custom-call(f32[4,24,1152]{2,1,0:T(8,128)S(1)} %copy-done.2, f32[4,24,1152]{2,1,0:T(8,128)S(1)} %copy-done.3, f32[4,24,1152]{2,1,0:T(8,128)S(1)} %copy-done.4, f32[4,24,1152]{2,1,0:T(8,128)S(1)} %copy-done.6, f32[4,24,1152]{2,1,0:T(8,128)S(1)} %copy-done.5, ...), custom_call_target="tpu_custom_call" | custom-call | tf_op jit(solution)/shard_map/update/pallas_call | solution.py:454
  42.9 0.0 copy-start.8
  42.9 41.1 %exchange.1 = (f32[8,328,128]{2,1,0:T(8,128)S(1)}, f32[4,8,8,128]{3,2,1,0:T(8,128)S(1)}) custom-call(f32[8,328,128]{2,1,0:T(8,128)S(1)} %get-tuple-element.7.send_ref, f32[8,128]{1,0:T(8,128)S(1)} %get-tuple-element.8.part_ref), custom_call_target="tpu_custom_call" | custom-call | tf_op jit(solution)/shard_map/exchange/pallas_call | solution.py:475
  84.0 0.0 copy-done.8
  84.0 10.0 %remap.1 = (f32[16,48,144]{2,1,0:T(8,128)}, f32[16,48,144]{2,1,0:T(8,128)}, f32[16,48,144]{2,1,0:T(8,128)}) custom-call(f32[8,328,128]{2,1,0:T(8,128)S(1)} %get-tuple-element.9.got_ref, f32[4,8,8,128]{3,2,1,0:T(8,128)S(1)} %get-tuple-element.10.sums_ref, f32[16]{0:T(128)S(1)} %copy-done.8, f32[1]{0:T(128)S(6)} %copy.15.target_ref), custom_call_target="tpu_custom_call" | custom-call | tf_op jit(solution)/shard_map/remap/pallas_call | solution.py:498
  (10 shorter events, 0.0 us)
Async XLA Ops:
  3.8 11.2 %collective-permute-start = (f32[4,4,1152]{2,1,0:T(4,128)S(1)}, f32[4,4,1152]{2,1,0:T(4,128)S(1)}, u32[]{:S(2)}, u32[]{:S(2)}) collective-permute-start(f32[4,4,1152]{2,1,0:T(4,128)S(1)} %pad_maximum_fusion), channel_id=1, source_target_pairs={{0,4},{4,8},{8,12},{12,16},{16,20},{20,24},{24,28},{1,5},{5,9},{9,... | collective-permute-start | bytes 221192 | tf_op jit(solution)/shard_map/ppermute | solution.py:446
  8.8 6.2 %collective-permute-start.1 = (f32[4,3,1152]{2,1,0:T(4,128)S(1)}, f32[4,3,1152]{2,1,0:T(4,128)S(1)}, u32[]{:S(2)}, u32[]{:S(2)}) collective-permute-start(f32[4,3,1152]{2,1,0:T(4,128)S(1)} %pad_maximum_fusion.1), channel_id=1, source_target_pairs={{4,0},{8,4},{12,8},{16,12},{20,16},{24,20},{28,24},{5,1},{9,5},{13... | collective-permute-start | bytes 165896 | tf_op jit(solution)/shard_map/ppermute | solution.py:447
  15.0 1.1 %copy-start = (bf16[5,256,256]{2,1,0:T(8,128)(2,1)S(1)}, bf16[5,256,256]{2,1,0:T(8,128)(2,1)}, u32[]{:S(2)}) copy-start(bf16[5,256,256]{2,1,0:T(8,128)(2,1)} %constant.8.clone.ml_ref) | copy-start | bytes 1966084
  16.1 1.1 %copy-start.1 = (bf16[5,256,256]{2,1,0:T(8,128)(2,1)S(1)}, bf16[5,256,256]{2,1,0:T(8,128)(2,1)}, u32[]{:S(2)}) copy-start(bf16[5,256,256]{2,1,0:T(8,128)(2,1)} %constant.7.clone.mh_ref) | copy-start | bytes 1966084
  17.2 1.0 %copy-start.2 = (f32[4,24,1152]{2,1,0:T(8,128)S(1)}, f32[4,24,1152]{2,1,0:T(8,128)}, u32[]{:S(2)}) copy-start(f32[4,24,1152]{2,1,0:T(8,128)} %p_ref.1) | copy-start | bytes 1327108
  18.2 1.0 %copy-start.3 = (f32[4,24,1152]{2,1,0:T(8,128)S(1)}, f32[4,24,1152]{2,1,0:T(8,128)}, u32[]{:S(2)}) copy-start(f32[4,24,1152]{2,1,0:T(8,128)} %t_ref.1) | copy-start | bytes 1327108
  19.2 1.0 %copy-start.4 = (f32[4,24,1152]{2,1,0:T(8,128)S(1)}, f32[4,24,1152]{2,1,0:T(8,128)}, u32[]{:S(2)}) copy-start(f32[4,24,1152]{2,1,0:T(8,128)} %q_ref.1) | copy-start | bytes 1327108
  20.3 1.0 %copy-start.5 = (f32[4,24,1152]{2,1,0:T(8,128)S(1)}, f32[4,24,1152]{2,1,0:T(8,128)}, u32[]{:S(2)}) copy-start(f32[4,24,1152]{2,1,0:T(8,128)} %n_ref.1) | copy-start | bytes 1327108
  21.3 1.0 %copy-start.6 = (f32[4,24,1152]{2,1,0:T(8,128)S(1)}, f32[4,24,1152]{2,1,0:T(8,128)}, u32[]{:S(2)}) copy-start(f32[4,24,1152]{2,1,0:T(8,128)} %e_ref.1) | copy-start | bytes 1327108
  22.3 0.9 copy-start.7
  23.2 0.7 copy-start.9
  23.8 0.7 copy-start.10
  42.9 41.2 %copy-start.8 = (f32[16]{0:T(128)S(1)}, f32[16]{0:T(128)}, u32[]{:S(2)}) copy-start(f32[16]{0:T(128)} %weight_ref.1) | copy-start | bytes 196
where the time goes:
time: 95.7 us; the launch traced here: 94 us
  Pallas kernels  69.5 us (73%)
  local copies, waits for them, and re-layouts  12.6 us (13%)
  starting transfers between devices  6.17 us (6%)
  waiting for transfers between devices  4.3 us (4%)
  between operations  1.35 us (1%)
    pallas_call x1, Pallas kernels, on_device(): pl.pallas_call(functools.partial(exchange_kernel, n_lat, n_lev), out_shap...  41.1 us
    pallas_call x1, Pallas kernels, on_device(): pl.pallas_call(functools.partial(update_kernel, n_lat), out_shape=(jax.Sh...  18.4 us
    pallas_call x1, Pallas kernels, on_device(): pl.pallas_call(functools.partial(remap_kernel, n_lat, n_lev, lats, nlon,...  9.99 us
    unnamed x22, local copies, waits for them, and re-layouts  9.45 us
    ppermute x1, starting transfers between devices, on_device(): south = lax.ppermute(tail, 'lat', [(i, i + 1) for i in range(n_lat - 1)])  4.87 us
    ppermute x1, waiting for transfers between devices, on_device(): north = lax.ppermute(head, 'lat', [(i + 1, i) for i in range(n_lat - 1)])  4.3 us
    slice x2, local copies, waits for them, and re-layouts, on_device(): head = jnp.stack([p[:, 0], t[:, 0], q[:, 0]], axis=1)  2.19 us
  transfers between devices with their start and end apart: 2, of which 1 were waited for; matrix products, arithmetic and copies ran while one was open for 0% of the time, Pallas kernels for 0%

commit v1 on v0

v1 whole, which is shorter than its diff:
```python
import functools
import math

import jax
import jax.numpy as jnp
import numpy as np
from jax import lax
from jax.experimental import pallas as pl
from jax.experimental.pallas import tpu as pltpu
from jax.sharding import PartitionSpec as P

LANES = 128
SUB = 8
VMEM = pl.BlockSpec(memory_space=pltpu.VMEM)
SMEM = pl.BlockSpec(memory_space=pltpu.SMEM)
MESH = pl.DeviceIdType.MESH


@functools.cache
def dft_tables(nlon):
    radix = nlon // LANES
    b = np.arange(LANES)[:, None]
    k2 = np.arange(LANES)[None, :]
    high, low = [], []
    for k1 in range(radix // 2 + 1):
        phase = (b * (k1 + radix * k2) % nlon) * (2.0 * np.pi / nlon)
        c, s = np.cos(phase), np.sin(phase)
        table = np.block([[c, -s], [s, c]]).astype(np.float32)
        top = table.astype(jnp.bfloat16)
        high.append(top)
        low.append((table - top.astype(np.float32)).astype(jnp.bfloat16))
    return np.stack(high), np.stack(low)


@functools.cache
def row_tables(nlat):
    rows = np.arange(nlat, dtype=np.float64)
    out = np.zeros((nlat, LANES), np.float32)
    out[:, 0] = np.sin((rows + 0.5) * np.pi / nlat)
    out[:, 1] = 1.0 / np.sin((rows + 0.5) * np.pi / nlat)
    out[:, 2] = np.sin((rows + 1.0) * np.pi / nlat)
    out[:, 3] = np.sin(rows * np.pi / nlat)
    return out


def pack_plan(width, groups):
    full, rest = divmod(width, LANES)
    cap = LANES // rest if rest else 1
    tail_tiles = -(-groups // cap) if rest else 0
    return full, rest, cap, tail_tiles


def split_bf16(x):
    top = x.astype(jnp.bfloat16)
    return top, (x - top.astype(jnp.float32)).astype(jnp.bfloat16)


def step_kernel(
    n_lat, n_lev, chunks,
    p_hbm, t_hbm, q_hbm, e_hbm, n_hbm, rows_hbm, mh_hbm, ml_hbm, mask_ref, cut_ref,
    out_ref, sums_ref,
    p_ref, t_ref, q_ref, e_ref, n_ref, rows_ref, mh_ref, ml_ref,
    last, head_rows, tail, head, south_ref, north_ref, tend, spec, new, yh, yl,
    send_ref, part_ref, mid,
    ins, edge, send_sem, recv_sem, s1, r1, s2, r2, local, sa, ra, sb, rb,
):
    levs, lats, nlon = p_hbm.shape
    i = lax.axis_index("lat")
    l = lax.axis_index("lev")
    barrier = pltpu.get_barrier_semaphore()

    for d in range(1, n_lat):
        pl.semaphore_signal(barrier, 1, device_id=((i + d) % n_lat, l), device_id_type=MESH)
    for d in range(1, n_lev):
        pl.semaphore_signal(barrier, 1, device_id=(i, (l + d) % n_lev), device_id_type=MESH)

    edges = []
    for f, ref in enumerate((p_hbm, t_hbm, q_hbm, n_hbm)):
        edges.append(pltpu.make_async_copy(ref.at[:, lats - SUB :, :], last.at[f], edge.at[0, f]))
    for f, ref in enumerate((p_hbm, t_hbm, q_hbm)):
        edges.append(pltpu.make_async_copy(ref.at[:, :SUB, :], head_rows.at[f], edge.at[1, f]))
    for copy in edges:
        copy.start()
    pairs = (
        (p_hbm, p_ref), (t_hbm, t_ref), (q_hbm, q_ref), (e_hbm, e_ref), (n_hbm, n_ref),
        (rows_hbm, rows_ref), (mh_hbm, mh_ref), (ml_hbm, ml_ref),
    )
    loads = [pltpu.make_async_copy(a, b, ins.at[c]) for c, (a, b) in enumerate(pairs)]
    for copy in loads:
        copy.start()
    for copy in edges:
        copy.wait()
    for f in range(4):
        for lev in range(levs):
            tail[lev, f : f + 1, :] = last[f, lev, SUB - 1 : SUB, :]
    for f in range(3):
        for lev in range(levs):
            head[lev, f : f + 1, :] = head_rows[f, lev, 0:1, :]
    for lev in range(levs):
        head[lev, 3:4, :] = jnp.zeros((1, nlon), jnp.float32)

    def send(src, dst, c, to):
        return pltpu.make_async_remote_copy(
            src_ref=src, dst_ref=dst, send_sem=send_sem.at[c], recv_sem=recv_sem.at[c],
            device_id=(to, l), device_id_type=MESH,
        )

    pl.semaphore_wait(barrier, n_lat - 1 + n_lev - 1)

    @pl.when(i < n_lat - 1)
    def _():
        send(tail, south_ref, 0, i + 1).start()

    @pl.when(i > 0)
    def _():
        send(head, north_ref, 1, i - 1).start()

    @pl.when(i == 0)
    def _():
        south_ref[...] = jnp.zeros_like(south_ref)

    @pl.when(i == n_lat - 1)
    def _():
        north_ref[...] = jnp.zeros_like(north_ref)

    for copy in loads:
        copy.wait()

    @pl.when(i < n_lat - 1)
    def _():
        send(tail, south_ref, 0, i + 1).wait_send()
        send(head, north_ref, 1, i + 1).wait_recv()

    @pl.when(i > 0)
    def _():
        send(head, north_ref, 1, i - 1).wait_send()
        send(tail, south_ref, 0, i - 1).wait_recv()

    order = sorted(range(1, n_lat), key=lambda d: abs(d - n_lat / 2))
    per = n_lat // n_lev
    owner = i // per
    own_slot = l * per + i % per

    def remote(src, dst, ss, rs, dev):
        return pltpu.make_async_remote_copy(
            src_ref=src, dst_ref=dst, send_sem=ss, recv_sem=rs, device_id=dev, device_id_type=MESH
        )

    def stage1(d, c, direct):
        dst = out_ref.at[own_slot, c] if direct else mid.at[d, c]
        j = (i + d) % n_lat
        return remote(send_ref.at[j, c], dst, s1.at[d, c], r1.at[d, c], (j, l))

    def stage2(d, c, src_lat, src):
        slot = l * per + src_lat % per
        return remote(src, out_ref.at[slot, c], s2.at[d, c], r2.at[slot, c], (i, src_lat // per))

    def own_block(c):
        return pltpu.make_async_copy(send_ref.at[i, c], out_ref.at[own_slot, c], local.at[c])

    def sums_a(d):
        j = (i + d) % n_lat
        return remote(part_ref, sums_ref.at[l, i], sa.at[d], ra.at[d], (j, l))

    def sums_b(d):
        return remote(sums_ref.at[l], sums_ref.at[l], sb.at[d], rb.at[d], (i, (l + d) % n_lev))

    radix = nlon // LANES
    half = radix // 2
    first = pl.multiple_of(lax.axis_index("lat") * lats, SUB)
    table = rows_ref[pl.ds(first, lats), :]
    cc, icc, face, face_s = (table[:, c : c + 1] for c in range(4))
    face_s = face_s[0:1]
    row = lax.broadcasted_iota(jnp.int32, (lats, nlon), 0)

    def up(x, halo):
        return jnp.where(row == lats - 1, halo, pltpu.roll(x, lats - 1, 0))

    def down(x, halo):
        return jnp.where(row == 0, halo, pltpu.roll(x, 1, 0))

    def east(x):
        return pltpu.roll(x, nlon - 1, 1)

    def west(x):
        return pltpu.roll(x, 1, 1)

    clevs = levs // chunks
    sub_row = lax.broadcasted_iota(jnp.int32, (lats, 2 * LANES), 0)
    cuts = jnp.full((lats, 2 * LANES), nlon, jnp.int32)
    for r in range(lats):
        value = jnp.where(mask_ref[r] > 0, cut_ref[r], nlon)
        cuts = jnp.where(sub_row == r, value, cuts)
    k2 = lax.broadcasted_iota(jnp.int32, (lats, 2 * LANES), 1) % LANES

    dot = functools.partial(jnp.dot, preferred_element_type=jnp.float32)

    def dot_t(a, b):
        return lax.dot_general(a, b, (((1,), (1,)), ((), ())), preferred_element_type=jnp.float32)

    part_ref[...] = jnp.zeros_like(part_ref)

    for chunk in range(chunks):
        @pl.loop(0, clevs)
        def _(cl):
            l = cl + chunk * clevs
            p, t, q, ec, nc = (r[l] for r in (p_ref, t_ref, q_ref, e_ref, n_ref))
            em = ec * (p + east(p)) * 0.5
            nm = nc * (p + up(p, north_ref[l, 0:1])) * 0.5 * face
            sm = south_ref[l, 3:4] * (south_ref[l, 0:1] + p[0:1]) * 0.5 * face_s
            base = pl.multiple_of(cl * 3 * lats, SUB)
            tend[pl.ds(base, lats)] = -((em - west(em)) + (nm - down(nm, sm)) * icc)
            for f, s in ((1, t), (2, q)):
                es = em * (s + east(s)) * 0.5
                ns = nm * (s + up(s, north_ref[l, f : f + 1])) * 0.5
                ss = sm * (south_ref[l, f : f + 1] + s[0:1]) * 0.5
                tend[pl.ds(pl.multiple_of(base + f * lats, SUB), lats)] = -(
                    (es - west(es)) + (ns - down(ns, ss)) * icc
                )

        total_rows = tend.shape[0]
        block = 48 if total_rows % 48 == 0 else 16

        @pl.loop(0, total_rows // block)
        def _(rb):
            at = pl.ds(pl.multiple_of(rb * block, 16), block)
            c = [tend[at, a * LANES : (a + 1) * LANES] for a in range(radix)]
            s = [c[a] + c[radix - a] for a in range(1, half + 1)]
            d = [c[a] - c[radix - a] for a in range(1, half + 1)]
            for k1 in range(half + 1):
                re = c[0]
                im = None
                for a in range(1, half + 1):
                    angle = 2.0 * math.pi * (a * k1 % radix) / radix
                    re = re + s[a - 1] * math.cos(angle)
                    if k1:
                        term = d[a - 1] * -math.sin(angle)
                        im = term if im is None else im + term
                lo = 0 if k1 == 0 else LANES + (k1 - 1) * 2 * LANES
                h, w = split_bf16(re)
                yh[at, lo : lo + LANES] = h
                yl[at, lo : lo + LANES] = w
                if k1:
                    h, w = split_bf16(im)
                    yh[at, lo + LANES : lo + 2 * LANES] = h
                    yl[at, lo + LANES : lo + 2 * LANES] = w

        for k1 in range(half + 1):
            lo = 0 if k1 == 0 else LANES + (k1 - 1) * 2 * LANES
            size = LANES if k1 == 0 else 2 * LANES
            mh, ml = mh_ref[k1, :size], ml_ref[k1, :size]
            h, w = yh[:, lo : lo + size], yl[:, lo : lo + size]
            x = dot(h, mh) + dot(h, ml) + dot(w, mh)
            k = k1 + radix * k2
            wave = jnp.minimum(k, nlon - k)
            keep = jnp.where(wave >= cuts, (1.0 if k1 == 0 else 2.0) / nlon, 0.0)
            x = (x.reshape(-1, lats, 2 * LANES) * keep[None]).reshape(-1, 2 * LANES)
            h, w = split_bf16(x)
            spec[:, lo : lo + size] = dot_t(h, mh) + dot_t(h, ml) + dot_t(w, mh)

        @pl.loop(0, clevs)
        def _(cl):
            l = cl + chunk * clevs
            base = pl.multiple_of(cl * 3 * lats, SUB)

            def filtered(f):
                at = pl.ds(pl.multiple_of(base + f * lats, SUB), lats)
                z0 = spec[at, 0:LANES]
                re = [spec[at, (2 * k - 1) * LANES : 2 * k * LANES] for k in range(1, half + 1)]
                im = [spec[at, 2 * k * LANES : (2 * k + 1) * LANES] for k in range(1, half + 1)]
                parts = [None] * radix
                for a in range(half + 1):
                    even, odd = z0, None
                    for k in range(1, half + 1):
                        angle = 2.0 * math.pi * (a * k % radix) / radix
                        even = even + re[k - 1] * math.cos(angle)
                        if a:
                            term = im[k - 1] * math.sin(angle)
                            odd = term if odd is None else odd + term
                    if a:
                        parts[a] = even - odd
                        parts[radix - a] = even + odd
                    else:
                        parts[0] = even
                return tend[at] - jnp.concatenate(parts, axis=1)

            p, t, q = p_ref[l], t_ref[l], q_ref[l]
            fm = filtered(0)
            np_ = p + fm
            inv = 1.0 / p
            new[pl.ds(base, lats)] = np_
            area = np_ * cc
            acc = part_ref[...]
            for g in range(lats // SUB):
                for a in range(radix):
                    acc = acc + area[g * SUB : (g + 1) * SUB, a * LANES : (a + 1) * LANES]
            part_ref[...] = acc
            for f, s in ((1, t), (2, q)):
                new[pl.ds(pl.multiple_of(base + f * lats, SUB), lats)] = s + (filtered(f) - s * fm) * inv

        width = nlon // n_lat
        groups = total_rows // SUB
        full, rest, cap, tail_tiles = pack_plan(width, groups)
        lane = lax.broadcasted_iota(jnp.int32, (SUB, LANES), 1)
        for j in range(n_lat):
            t0, off = divmod(width * j, LANES)
            nt = -(-(off + width) // LANES)
            acc = None
            for g in range(groups):
                x = new[g * SUB : (g + 1) * SUB, t0 * LANES : (t0 + nt) * LANES]
                if off:
                    x = pltpu.roll(x, nt * LANES - off, 1)
                for a in range(full):
                    send_ref[j, chunk, (a * groups + g) * SUB : (a * groups + g + 1) * SUB, :] = x[
                        :, a * LANES : (a + 1) * LANES
                    ]
                if rest:
                    slot = g % cap
                    y = x[:, full * LANES : (full + 1) * LANES]
                    if slot:
                        y = pltpu.roll(y, slot * rest, 1)
                    acc = y if slot == 0 else jnp.where(lane >= slot * rest, y, acc)
                    if slot == cap - 1 or g == groups - 1:
                        o = (full * groups + g // cap) * SUB
                        send_ref[j, chunk, o : o + SUB, :] = acc


        @pl.when(owner == l)
        def _():
            for d in order:
                stage1(d, chunk, True).start()
            own_block(chunk).start()

        @pl.when(owner != l)
        def _():
            for d in order:
                stage1(d, chunk, False).start()
            stage2(0, chunk, i, send_ref.at[i, chunk]).start()


    own_part = pltpu.make_async_copy(part_ref, sums_ref.at[l, i], local.at[chunks])
    own_part.start()
    for d in order:
        sums_a(d).start()
    for c in range(chunks):
        for d in order:
            src_lat = (i + n_lat - d) % n_lat
            stage1(d, c, False).wait_recv()

            @pl.when(src_lat // per != l)
            def _():
                stage2(d, c, src_lat, mid.at[d, c]).start()

        if c == 0:
            own_part.wait()
            for d in order:
                sums_a(d).wait_recv()
            for d in range(1, n_lev):
                sums_b(d).start()

    for e in range(1, n_lev):
        for r in range(per):
            slot = ((l + e) % n_lev) * per + r
            for c in range(chunks):
                remote(mid.at[0, c], out_ref.at[slot, c], s2.at[0, c], r2.at[slot, c], (i, l)).wait_recv()
    for d in range(1, n_lev):
        sums_b(d).wait_recv()

    for d in order:
        sums_a(d).wait_send()
        src_lat = (i + n_lat - d) % n_lat
        for c in range(chunks):
            stage1(d, c, False).wait_send()

        @pl.when(src_lat // per != l)
        def _():
            for c in range(chunks):
                stage2(d, c, src_lat, mid.at[d, c]).wait_send()

    for d in range(1, n_lev):
        sums_b(d).wait_send()

    @pl.when(owner == l)
    def _():
        for c in range(chunks):
            own_block(c).wait()

    @pl.when(owner != l)
    def _():
        for c in range(chunks):
            stage2(0, c, i, send_ref.at[i, c]).wait_send()


def remap_kernel(
    n_lat, n_lev, chunks, lats, nlon, area_total,
    got_hbm, sums_ref, weight_ref, target_ref,
    thick_out, temp_out, tracer_out,
    cols, share, res, got, thick_buf, temp_buf, tracer_buf, in_sem, out_sem,
):
    per = n_lat // n_lev
    levels = thick_out.shape[0]
    levs = levels // n_lev
    rgs = lats // SUB
    width = nlon // n_lat
    clevs = levs // chunks
    groups = clevs * 3 * rgs
    full, rest, cap, tail_tiles = pack_plan(width, groups)
    lane = lax.broadcasted_iota(jnp.int32, (SUB, LANES), 1)
    outs = (thick_buf, temp_buf, tracer_buf)
    finals = (thick_out, temp_out, tracer_out)
    loads = [
        pltpu.make_async_copy(got_hbm.at[slot], got.at[slot], in_sem.at[slot])
        for slot in range(n_lev * per)
    ]
    for copy in loads:
        copy.start()

    whole = jnp.full((SUB, LANES), weight_ref[0])
    for k in range(1, levels):
        whole = whole + weight_ref[k]
    run = jnp.zeros((SUB, LANES), jnp.float32)
    for k in range(levels):
        part = jnp.full((SUB, LANES), weight_ref[k]) / whole
        run = run + part
        share[0, k] = part
        share[1, k] = run
        share[2, k] = 1.0 / part
    sums = sums_ref[...].reshape(-1, SUB, LANES)
    total = jnp.sum(jnp.sum(sums, axis=0), keepdims=True)
    factor = jnp.full((1, 1), target_ref[0] * (nlon * area_total)) / total

    n_main = full * per * rgs
    col_groups = per * rgs
    for lev in range(n_lev):
        for rs in range(per):
            loads[lev * per + rs].wait()
        for ll in range(levs):
            c, cl = divmod(ll, clevs)
            for f in range(3):
                acc = None
                for rs in range(per):
                    for rg in range(rgs):
                        g = (cl * 3 + f) * rgs + rg
                        for a in range(full):
                            v = (a * per + rs) * rgs + rg
                            o = (a * groups + g) * SUB
                            cols[f, lev * levs + ll, v] = got[lev * per + rs, c, o : o + SUB, :]
                        if rest:
                            o = (full * groups + g // cap) * SUB
                            y = got[lev * per + rs, c, o : o + SUB, :]
                            cg = rs * rgs + rg
                            slot = cg % cap
                            shift = (slot - g % cap) * rest % LANES
                            if shift:
                                y = pltpu.roll(y, shift, 1)
                            acc = (
                                y if slot == 0
                                else jnp.where(lane >= slot * rest, y, acc)
                            )
                            if slot == cap - 1 or cg == col_groups - 1:
                                last = (slot + 1) * rest
                                if last < LANES:
                                    acc = jnp.where(lane < last, acc, 1.0)
                                cols[f, lev * levs + ll, n_main + cg // cap] = acc

    def remap(v, put):
        thick = [cols[0, m, v] for m in range(levels)]
        tops = []
        surface = jnp.zeros((SUB, LANES), jnp.float32)
        for m in range(levels):
            tops.append(surface)
            surface = surface + thick[m]
        inv = 1.0 / surface
        scale = surface * factor
        before = (jnp.zeros_like(surface), jnp.zeros_like(surface))
        for k in range(levels):
            bound = surface * share[1, k]
            ct = cq = None
            for m in range(levels):
                w = jnp.minimum(jnp.maximum(bound - tops[m], 0.0), thick[m])
                dt, dq = cols[1, m, v] * w, cols[2, m, v] * w
                ct, cq = (dt, dq) if m == 0 else (ct + dt, cq + dq)
            per_share = inv * share[2, k]
            put(k, scale * share[0, k], (ct - before[0]) * per_share, (cq - before[1]) * per_share)
            before = (ct, cq)

    if rest:
        n_tail = -(-col_groups // cap)

        @pl.loop(0, n_tail)
        def _(v):
            def put(k, *values):
                for f, x in enumerate(values):
                    res[f, k, v] = x

            remap(n_main + v, put)

        for cg in range(col_groups):
            @pl.loop(0, levels)
            def _(k):
                for f in range(3):
                    x = res[f, k, cg // cap]
                    if cg % cap:
                        x = pltpu.roll(x, LANES - (cg % cap) * rest, 1)
                    outs[f][k, cg * SUB : (cg + 1) * SUB, full * LANES : full * LANES + rest] = x[:, :rest]

    def finish(v):
        at = pl.ds(pl.multiple_of(v * SUB, SUB), SUB)
        return [
            pltpu.make_async_copy(outs[f].at[:, at, :], finals[f].at[:, at, :], out_sem.at[f, v])
            for f in range(3)
        ]

    for a in range(full):
        @pl.loop(0, col_groups)
        def _(v):
            at = pl.ds(pl.multiple_of(v * SUB, SUB), SUB)

            def put(k, *values):
                for ref, x in zip(outs, values):
                    ref[k, at, a * LANES : (a + 1) * LANES] = x

            remap(a * col_groups + v, put)
            if a == full - 1:
                for copy in finish(v):
                    copy.start()

    if not full:
        for v in range(col_groups):
            for copy in finish(v):
                copy.start()
    for v in range(col_groups):
        for copy in finish(v):
            copy.wait()


def on_device(p, t, q, ec, nc, polar_mask, wave_cutoff, level_weight, target_surface):
    levs, lats, nlon = p.shape
    n_lat, n_lev = lax.axis_size("lat"), lax.axis_size("lev")
    nlat = lats * n_lat
    levels = levs * n_lev
    per = n_lat // n_lev
    width = nlon // n_lat
    f32 = jnp.float32
    high, low = dft_tables(nlon)
    chunks = 2
    rows = levs * 3 * lats
    crows = rows // chunks
    groups = crows // SUB
    full, rest, cap, tail_tiles = pack_plan(width, groups)
    packed = (full * groups + tail_tiles) * SUB
    dma = pltpu.SemaphoreType.DMA
    grant = 62_800_000
    given = (p, t, q, ec, nc, jnp.asarray(row_tables(nlat)), jnp.asarray(high), jnp.asarray(low))
    hbm = pl.BlockSpec(memory_space=pltpu.HBM)
    got, sums = pl.pallas_call(
        functools.partial(step_kernel, n_lat, n_lev, chunks),
        out_shape=(
            jax.ShapeDtypeStruct((n_lat, chunks, packed, LANES), f32),
            jax.ShapeDtypeStruct((n_lev, n_lat, SUB, LANES), f32),
        ),
        in_specs=[hbm] * 8 + [SMEM] * 2,
        out_specs=(hbm, hbm),
        scratch_shapes=[pltpu.VMEM(x.shape, x.dtype) for x in given] + [
            pltpu.VMEM((4, levs, SUB, nlon), f32),
            pltpu.VMEM((3, levs, SUB, nlon), f32),
            pltpu.VMEM((levs, 4, nlon), f32),
            pltpu.VMEM((levs, 4, nlon), f32),
            pltpu.VMEM((levs, 4, nlon), f32),
            pltpu.VMEM((levs, 4, nlon), f32),
            pltpu.VMEM((crows, nlon), f32),
            pltpu.VMEM((crows, nlon), f32),
            pltpu.VMEM((crows, nlon), f32),
            pltpu.VMEM((crows, nlon), jnp.bfloat16),
            pltpu.VMEM((crows, nlon), jnp.bfloat16),
            pltpu.VMEM((n_lat, chunks, packed, LANES), f32),
            pltpu.VMEM((SUB, LANES), f32),
            pltpu.VMEM((n_lat, chunks, packed, LANES), f32),
            dma((8,)), dma((2, 4)), dma((2,)), dma((2,)),
            dma((n_lat, chunks)), dma((n_lat, chunks)), dma((n_lat, chunks)), dma((n_lat, chunks)),
            dma((chunks + 1,)), dma((n_lat,)), dma((n_lat,)), dma((n_lev,)), dma((n_lev,)),
        ],
        compiler_params=pltpu.CompilerParams(
            collective_id=0, has_side_effects=True, vmem_limit_bytes=grant
        ),
        name="step",
    )(*given, polar_mask, wave_cutoff)

    area_total = float(np.sum(np.sin((np.arange(nlat) + 0.5) * np.pi / nlat)))
    col_groups = per * lats // SUB
    n_tail = -(-col_groups // cap) if rest else 0
    out = jax.ShapeDtypeStruct((levels, nlat // n_lev, width), f32)
    return pl.pallas_call(
        functools.partial(remap_kernel, n_lat, n_lev, chunks, lats, nlon, area_total),
        out_shape=(out, out, out),
        in_specs=[hbm, VMEM, SMEM, SMEM],
        out_specs=(hbm, hbm, hbm),
        scratch_shapes=[
            pltpu.VMEM((3, levels, full * col_groups + n_tail, SUB, LANES), f32),
            pltpu.VMEM((3, levels, SUB, LANES), f32),
            pltpu.VMEM((3, levels, max(n_tail, 1), SUB, LANES), f32),
            pltpu.VMEM(got.shape, f32),
            pltpu.VMEM(out.shape, f32), pltpu.VMEM(out.shape, f32), pltpu.VMEM(out.shape, f32),
            dma((n_lat,)), dma((3, col_groups)),
        ],
        compiler_params=pltpu.CompilerParams(vmem_limit_bytes=grant),
        name="remap",
    )(got, sums, level_weight, target_surface)


def solution(mesh):
    return jax.shard_map(
        on_device,
        mesh=mesh,
        in_specs=(P("lev", "lat", None),) * 5 + (P("lat"), P("lat"), P(), P()),
        out_specs=(P(None, "lev", "lat"),) * 3,
        check_vma=False,
    )
```

time: 95.7 us -> 73.8 us (0.77); the launches traced: 94 us -> 73.6 us
  local copies, waits for them, and re-layouts: 12.6 us -> 0 us
  starting transfers between devices: 6.17 us -> 0 us
  waiting for transfers between devices: 4.3 us -> 0 us
  Pallas kernels: 69.5 us -> 72.3 us
    unnamed x22 -> x0, local copies, waits for them, and re-layouts: 9.45 us -> none
    ppermute x2 -> x0, starting transfers between devices: 6.17 us -> none  [the longest x1 4.87 us: on_device(): south = lax.ppermute(tail, 'lat', [(i, i + 1) for i in range(n_lat - 1)])]
    ppermute x2 -> x0, waiting for transfers between devices: 4.3 us -> none  [the longest x1 4.3 us: on_device(): north = lax.ppermute(head, 'lat', [(i + 1, i) for i in range(n_lat - 1)])]
    slice x3 -> x0, local copies, waits for them, and re-layouts: 3.12 us -> none  [the longest x2 2.19 us: on_device(): head = jnp.stack([p[:, 0], t[:, 0], q[:, 0]], axis=1)]
    pallas_call x3 -> x2, Pallas kernels: 69.5 us -> 72.3 us  [the longest x1 61.2 us: on_device(): pl.pallas_call(functools.partial(step_kernel, n_lat, n_lev, chunks), out_...]
  transfers between devices with their start and end apart: 2 -> 0, of which waited for: 1 -> 0; matrix products, arithmetic and copies ran while one was open for 0% -> 0% of each run, Pallas kernels for 0% -> 0%
where the time goes in v1:
time: 73.8 us; the launch traced here: 73.6 us
  Pallas kernels  72.3 us (98%)
  between operations  1.29 us (2%)
    pallas_call x1, Pallas kernels, on_device(): pl.pallas_call(functools.partial(step_kernel, n_lat, n_lev, chunks), out_...  61.2 us
    pallas_call x1, Pallas kernels, on_device(): pl.pallas_call(functools.partial(remap_kernel, n_lat, n_lev, chunks, lats...  11.1 us

profile of v1, /device:TPU:0, one launch (start us, length us, event | category | flops | bytes accessed | tf_op | source)
XLA Modules:
  0.0 73.6 jit_solution(8649279004445636956)
XLA Ops:
  1.3 61.2 %step.1 = (f32[8,2,168,128]{3,2,1,0:T(8,128)}, f32[4,8,8,128]{3,2,1,0:T(8,128)}) custom-call(f32[4,24,1152]{2,1,0:T(8,128)} %p_hbm.1, f32[4,24,1152]{2,1,0:T(8,128)} %t_hbm.1, f32[4,24,1152]{2,1,0:T(8,128)} %q_hbm.1, f32[4,24,1152]{2,1,0:T(8,128)} %e_hbm.1, f32[4,24,1152]{2,1,0:T(8,128)} %n_hbm.1, f32[192,128]{1,0:T(8,128)} %constant.6.clone.rows_hbm, ...), custom_call_target="tpu_custom_call" | custom-call | tf_op jit(solution)/shard_map/step/pallas_call | solution.py:556
  62.5 11.1 %remap.1 = (f32[16,48,144]{2,1,0:T(8,128)}, f32[16,48,144]{2,1,0:T(8,128)}, f32[16,48,144]{2,1,0:T(8,128)}) custom-call(f32[8,2,168,128]{3,2,1,0:T(8,128)} %get-tuple-element.5.got_hbm, f32[4,8,8,128]{3,2,1,0:T(8,128)} %get-tuple-element.6.sums_ref, f32[16]{0:T(128)} %weight_ref.1, f32[1]{0:T(128)S(6)} %copy.15.target_ref), custom_call_target="tpu_custom_call" | custom-call | tf_op jit(solution)/shard_map/remap/pallas_call | solution.py:593

commit v2 on v1

--- a/solution.py
+++ b/solution.py
@@ -307,18 +307,24 @@
             nt = -(-(off + width) // LANES)
             acc = None
             for g in range(groups):
-                x = new[g * SUB : (g + 1) * SUB, t0 * LANES : (t0 + nt) * LANES]
-                if off:
-                    x = pltpu.roll(x, nt * LANES - off, 1)
+                def piece(a):
+                    t, cut = divmod(width * j + a * LANES, LANES)
+                    wide = LANES if a < full else rest
+                    at = slice(g * SUB, (g + 1) * SUB)
+                    x = new[at, t * LANES : (t + 1) * LANES]
+                    if cut + wide > LANES:
+                        y = new[at, (t + 1) * LANES : (t + 2) * LANES]
+                        x = jnp.where(lane >= cut, x, y)
+                    return x
+
                 for a in range(full):
-                    send_ref[j, chunk, (a * groups + g) * SUB : (a * groups + g + 1) * SUB, :] = x[
-                        :, a * LANES : (a + 1) * LANES
-                    ]
+                    o = (a * groups + g) * SUB
+                    send_ref[j, chunk, o : o + SUB, :] = piece(a)
                 if rest:
                     slot = g % cap
-                    y = x[:, full * LANES : (full + 1) * LANES]
-                    if slot:
-                        y = pltpu.roll(y, slot * rest, 1)
+                    y = piece(full)
+                    if (slot * rest - off) % LANES:
+                        y = pltpu.roll(y, (slot * rest - off) % LANES, 1)
                     acc = y if slot == 0 else jnp.where(lane >= slot * rest, y, acc)
                     if slot == cap - 1 or g == groups - 1:
                         o = (full * groups + g // cap) * SUB
@@ -407,6 +413,7 @@
     full, rest, cap, tail_tiles = pack_plan(width, groups)
     lane = lax.broadcasted_iota(jnp.int32, (SUB, LANES), 1)
     outs = (thick_buf, temp_buf, tracer_buf)
+    turn = (LANES - lax.axis_index("lat") * width % LANES) % LANES
     finals = (thick_out, temp_out, tracer_out)
     loads = [
         pltpu.make_async_copy(got_hbm.at[slot], got.at[slot], in_sem.at[slot])
@@ -518,6 +525,7 @@
 
             def put(k, *values):
                 for ref, x in zip(outs, values):
+                    x = pltpu.roll(x, turn, 1)
                     ref[k, at, a * LANES : (a + 1) * LANES] = x
 
             remap(a * col_groups + v, put)

time: 73.8 us -> 69.3 us (0.939)
  Pallas kernels: 72.3 us -> 67.8 us
    pallas_call x1, Pallas kernels: 61.2 us -> 56.3 us  [on_device(): pl.pallas_call(functools.partial(step_kernel, n_lat, n_lev, chunks), out_...]
where the time goes in v2:
time: 69.3 us; the launch traced here: 69.1 us
  Pallas kernels  67.8 us (98%)
  between operations  1.29 us (2%)
    pallas_call x1, Pallas kernels, on_device(): pl.pallas_call(functools.partial(step_kernel, n_lat, n_lev, chunks), out_...  56.3 us
    pallas_call x1, Pallas kernels, on_device(): pl.pallas_call(functools.partial(remap_kernel, n_lat, n_lev, chunks, lats...  11.5 us

profile of v2, /device:TPU:0, one launch (start us, length us, event | category | flops | bytes accessed | tf_op | source)
XLA Modules:
  0.0 69.1 jit_solution(12558818741045420448)
XLA Ops:
  1.3 56.3 %step.1 = (f32[8,2,168,128]{3,2,1,0:T(8,128)}, f32[4,8,8,128]{3,2,1,0:T(8,128)}) custom-call(f32[4,24,1152]{2,1,0:T(8,128)} %p_hbm.1, f32[4,24,1152]{2,1,0:T(8,128)} %t_hbm.1, f32[4,24,1152]{2,1,0:T(8,128)} %q_hbm.1, f32[4,24,1152]{2,1,0:T(8,128)} %e_hbm.1, f32[4,24,1152]{2,1,0:T(8,128)} %n_hbm.1, f32[192,128]{1,0:T(8,128)} %constant.6.clone.rows_hbm, ...), custom_call_target="tpu_custom_call" | custom-call | tf_op jit(solution)/shard_map/step/pallas_call | solution.py:564
  57.6 11.5 %remap.1 = (f32[16,48,144]{2,1,0:T(8,128)}, f32[16,48,144]{2,1,0:T(8,128)}, f32[16,48,144]{2,1,0:T(8,128)}) custom-call(f32[8,2,168,128]{3,2,1,0:T(8,128)} %get-tuple-element.5.got_hbm, f32[4,8,8,128]{3,2,1,0:T(8,128)} %get-tuple-element.6.sums_ref, f32[16]{0:T(128)} %weight_ref.1, f32[1]{0:T(128)S(6)} %copy.15.target_ref), custom_call_target="tpu_custom_call" | custom-call | tf_op jit(solution)/shard_map/remap/pallas_call | solution.py:601
